TPU v7x, 32 devices: a whole 2x2x4 slice. The times are simulated.
32 devices in a mesh: seq: 8 (over y, x, core), rep: 4 (over z).
Axes of the slice: x: 2, y: 2, z: 4, core: 2. Of those that a mesh axis runs over, the one named last changes fastest.
Arguments:
- query_rows: bfloat16 [8, 8, 256, 1152], P('rep', 'seq'), as said below
- key_rows: bfloat16 [8, 8, 256, 1152], P('rep', 'seq'), as said below
- value_rows: bfloat16 [8, 8, 256, 1152], P('rep', 'seq'), may hold values from -6 to 6
- out_grad: bfloat16 [8, 8, 256, 1152], P('rep', 'seq'), may hold values from -6 to 6
- out_weight: bfloat16 [1152, 1152], replicated, may hold values from -0.1875 to 0.1875
- frame_count: int32 [8], P('rep'), may hold values from 1 to 8, as said below
- pos_count: int32 [8], P('rep'), may hold values from 64 to 256, as said below
Outputs:
- projected: bfloat16 [8, 8, 256, 1152], P('rep', 'seq')
- grad_query: bfloat16 [8, 8, 256, 1152], P('rep', 'seq')
- grad_key: bfloat16 [8, 8, 256, 1152], P('rep', 'seq')
- grad_value: bfloat16 [8, 8, 256, 1152], P('rep', 'seq')
- grad_weight: float32 [1152, 1152], P('seq')
Inputs may be any that keep to these rules, and one draw needn't show every extreme that they name: `query_rows`: entries lie within -40 to 40. `key_rows`: entries lie within -40 to 40. `frame_count`: some clip has all 8 frames live. `pos_count`: some clip has all 256 positions live.
All inputs are finite; a program needn't handle non-finite values.
Results may differ from a plain program's by a relative error of at most 0.0057.
Values may be sent and summed in bfloat16 or wider, within the bound.
No kernel may reach another device: no remote copies, remote signals or barrier semaphores. Data moves between devices by JAX's collectives and lax.ppermute only.
A program may use at most 128 MiB of HBM per device.

v0:
```python
import math
import jax
import jax.numpy as jnp
from jax import lax
from jax.sharding import PartitionSpec as P

HEADS = 16


def attend_local(query_part, key_part, value_part, key_live, row_live):
    nframe, npos_part, width = query_part.shape
    head_dim = width // HEADS
    inv_root = 1.0 / math.sqrt(head_dim)
    shape_heads = (nframe, npos_part, HEADS, head_dim)
    query_heads = query_part.reshape(shape_heads)
    key_heads = key_part.reshape(shape_heads)
    value_heads = value_part.reshape(shape_heads)
    scores = (
        jnp.einsum("fphd,tphd->phft", query_heads, key_heads, preferred_element_type=jnp.float32)
        * inv_root
    )
    scores = jnp.where(key_live, scores, -1e30)
    highest = jnp.max(scores, axis=-1, keepdims=True)
    expo = jnp.exp(scores - highest) * key_live.astype(jnp.float32)
    weights = expo / jnp.sum(expo, axis=-1, keepdims=True)
    rounded = weights.astype(jnp.bfloat16)
    mixed = jnp.einsum("phft,tphd->fphd", rounded, value_heads, preferred_element_type=jnp.float32)
    attn_out = jnp.where(row_live[:, :, None], mixed.reshape(nframe, npos_part, width), 0.0).astype(
        jnp.bfloat16
    )
    return (attn_out, weights, rounded)


def attend_back(query_part, key_part, value_part, cot_part, weights, rounded):
    nframe, npos_part, width = query_part.shape
    head_dim = width // HEADS
    inv_root = 1.0 / math.sqrt(head_dim)
    shape_heads = (nframe, npos_part, HEADS, head_dim)
    cot_heads = cot_part.reshape(shape_heads)
    value_heads = value_part.reshape(shape_heads)
    grad_value = jnp.einsum(
        "phft,fphd->tphd", rounded, cot_heads, preferred_element_type=jnp.float32
    )
    grad_attn = jnp.einsum(
        "fphd,tphd->phft", cot_heads, value_heads, preferred_element_type=jnp.float32
    )
    row_delta = jnp.sum(weights * grad_attn, axis=-1, keepdims=True)
    grad_score = weights * (grad_attn - row_delta) * inv_root
    key_wide = key_part.astype(jnp.float32).reshape(shape_heads)
    query_wide = query_part.astype(jnp.float32).reshape(shape_heads)
    grad_query = jnp.einsum(
        "phft,tphd->fphd", grad_score, key_wide, precision=lax.Precision.HIGHEST
    )
    grad_key = jnp.einsum(
        "phft,fphd->tphd", grad_score, query_wide, precision=lax.Precision.HIGHEST
    )
    full = (nframe, npos_part, width)
    return (
        grad_query.reshape(full).astype(jnp.bfloat16),
        grad_key.reshape(full).astype(jnp.bfloat16),
        grad_value.reshape(full).astype(jnp.bfloat16),
    )


def reduce_weight(flat_grad, flat_out):
    mine = lax.psum_scatter(
        lax.dot_general(
            flat_grad, flat_out, (((0,), (0,)), ((), ())), preferred_element_type=jnp.float32
        ),
        "seq",
        scatter_dimension=0,
        tiled=True,
    )
    return lax.psum(mine, "rep")


def shards(query_rows, key_rows, value_rows, out_grad, out_weight, frame_count, pos_count):
    clip_local, frame_local, npos_all, width = query_rows.shape
    rank = lax.axis_index("seq")
    query_pos, key_pos, value_pos = (
        lax.all_to_all(query_rows, "seq", split_axis=2, concat_axis=1, tiled=True),
        lax.all_to_all(key_rows, "seq", split_axis=2, concat_axis=1, tiled=True),
        lax.all_to_all(value_rows, "seq", split_axis=2, concat_axis=1, tiled=True),
    )
    nframe = query_pos.shape[1]
    npos_part = query_pos.shape[2]
    frame_ids = jnp.arange(nframe, dtype=jnp.int32)
    position_ids = rank * npos_part + jnp.arange(npos_part, dtype=jnp.int32)
    key_live = frame_ids[None, :] < frame_count[:, None]
    row_live = key_live[:, :, None] & (position_ids[None, None, :] < pos_count[:, None, None])
    attn_pos, weights, rounded = jax.vmap(attend_local)(
        query_pos, key_pos, value_pos, key_live, row_live
    )
    attn_frames = lax.all_to_all(attn_pos, "seq", split_axis=1, concat_axis=2, tiled=True)
    flat_out = attn_frames.reshape(-1, width)
    flat_grad = out_grad.reshape(-1, width)
    projected = lax.dot_general(
        flat_out, out_weight, (((1,), (1,)), ((), ())), preferred_element_type=jnp.float32
    )
    projected = projected.astype(jnp.bfloat16).reshape(query_rows.shape)
    own_frames = rank * frame_local + jnp.arange(frame_local, dtype=jnp.int32)
    frame_alive = own_frames[None, :, None] < frame_count[:, None, None]
    place_alive = jnp.arange(npos_all, dtype=jnp.int32)[None, None, :] < pos_count[:, None, None]
    out_cot = jnp.dot(flat_grad, out_weight, preferred_element_type=jnp.float32).reshape(
        query_rows.shape
    )
    out_cot = jnp.where((frame_alive & place_alive)[..., None], out_cot, 0.0).astype(jnp.bfloat16)
    cot_pos = lax.all_to_all(out_cot, "seq", split_axis=2, concat_axis=1, tiled=True)
    grad_query_pos, grad_key_pos, grad_value_pos = jax.vmap(attend_back)(
        query_pos, key_pos, value_pos, cot_pos, weights, rounded
    )
    grad_query, grad_key, grad_value = (
        lax.all_to_all(grad_query_pos, "seq", split_axis=1, concat_axis=2, tiled=True),
        lax.all_to_all(grad_key_pos, "seq", split_axis=1, concat_axis=2, tiled=True),
        lax.all_to_all(grad_value_pos, "seq", split_axis=1, concat_axis=2, tiled=True),
    )
    grad_weight = reduce_weight(flat_grad, flat_out)
    return (projected, grad_query, grad_key, grad_value, grad_weight)


def solution(mesh):
    in_specs = (
        P("rep", "seq", None, None),
        P("rep", "seq", None, None),
        P("rep", "seq", None, None),
        P("rep", "seq", None, None),
        P(),
        P("rep"),
        P("rep"),
    )
    out_specs = (
        P("rep", "seq", None, None),
        P("rep", "seq", None, None),
        P("rep", "seq", None, None),
        P("rep", "seq", None, None),
        P("seq", None),
    )
    return jax.shard_map(shards, mesh=mesh, in_specs=in_specs, out_specs=out_specs, check_vma=False)
```

profile of v0, /device:TPU:0, one launch (start us, length us, event | category | flops | bytes accessed | tf_op | source)
XLA Modules:
  0.0 298.1 jit_solution(12987899901119479207)
XLA Ops:
  7.2 0.0 copy-start
  7.2 3.6 %copy.97 = bf16[2,1,256,1152]{3,0,1,2:T(2,128)(2,1)} copy(bf16[2,1,256,1152]{3,2,1,0:T(8,128)(2,1)} %param.7) | data formatting | bytes 2359296 | tf_op args[0]
  10.8 5.2 %all-to-all-start = ((bf16[2,1,256,1152]{3,0,1,2:T(2,128)(2,1)}), bf16[2,1,256,1152]{3,0,1,2:T(2,128)(2,1)}, u32[]{:S(2)}, u32[]{:S(2)}) async-start(bf16[2,1,256,1152]{3,0,1,2:T(2,128)(2,1)} %copy.97), calls=%async_computation | async-start | bytes 2359296 | tf_op jit(solution)/shard_map/all_to_all | solution.py:81
  16.0 3.5 %copy.99 = bf16[2,1,256,1152]{3,0,1,2:T(2,128)(2,1)} copy(bf16[2,1,256,1152]{3,2,1,0:T(8,128)(2,1)} %param.8) | data formatting | bytes 2359296 | tf_op args[1]
  19.5 13.4 %all-to-all-done = bf16[2,1,256,1152]{3,0,1,2:T(2,128)(2,1)} async-done(((bf16[2,1,256,1152]{3,0,1,2:T(2,128)(2,1)}), bf16[2,1,256,1152]{3,0,1,2:T(2,128)(2,1)}, u32[]{:S(2)}, u32[]{:S(2)}) %all-to-all-start) | async-done | bytes 1179680 | tf_op jit(solution)/shard_map/all_to_all | solution.py:81
  32.9 4.3 %all-to-all-start.1 = ((bf16[2,1,256,1152]{3,0,1,2:T(2,128)(2,1)}), bf16[2,1,256,1152]{3,0,1,2:T(2,128)(2,1)}, u32[]{:S(2)}, u32[]{:S(2)}) async-start(bf16[2,1,256,1152]{3,0,1,2:T(2,128)(2,1)} %copy.99), calls=%async_computation.1 | async-start | bytes 2359296 | tf_op jit(solution)/shard_map/all_to_all | solution.py:82
  37.2 0.0 copy-start.6
  37.2 0.0 copy-start.5
  37.2 3.5 %copy.103 = bf16[2,1,256,1152]{3,0,1,2:T(2,128)(2,1)} copy(bf16[2,1,256,1152]{3,2,1,0:T(8,128)(2,1)} %param.9) | data formatting | bytes 2359296 | tf_op args[2]
  40.7 13.3 %all-to-all-done.1 = bf16[2,1,256,1152]{3,0,1,2:T(2,128)(2,1)} async-done(((bf16[2,1,256,1152]{3,0,1,2:T(2,128)(2,1)}), bf16[2,1,256,1152]{3,0,1,2:T(2,128)(2,1)}, u32[]{:S(2)}, u32[]{:S(2)}) %all-to-all-start.1) | async-done | bytes 1179680 | tf_op jit(solution)/shard_map/all_to_all | solution.py:82
  54.0 4.2 %all-to-all-start.2 = ((bf16[2,1,256,1152]{3,0,1,2:T(2,128)(2,1)}), bf16[2,1,256,1152]{3,0,1,2:T(2,128)(2,1)}, u32[]{:S(2)}, u32[]{:S(2)}) async-start(bf16[2,1,256,1152]{3,0,1,2:T(2,128)(2,1)} %copy.103), calls=%async_computation.2 | async-start | bytes 2359296 | tf_op jit(solution)/shard_map/all_to_all | solution.py:83
  58.2 0.6 reduce-scatter.4.cloned.1.call-start
  58.8 0.1 broadcast_compare_fusion
  58.9 0.1 iota_compare_fusion
  59.0 0.1 broadcast_and_fusion
  59.0 6.5 %reshape.214 = bf16[2,8,32,16,72]{4,3,0,2,1:T(8,128)(2,1)} reshape(bf16[2,1,256,1152]{3,0,1,2:T(2,128)(2,1)} %all-to-all-done) | data formatting | bytes 2359296 | tf_op jit(solution)/shard_map/vmap()/reshape | solution.py:15
  65.6 6.5 %reshape.215 = bf16[2,8,32,16,72]{4,3,0,2,1:T(8,128)(2,1)} reshape(bf16[2,1,256,1152]{3,0,1,2:T(2,128)(2,1)} %all-to-all-done.1) | data formatting | bytes 2359296 | tf_op jit(solution)/shard_map/vmap()/reshape | solution.py:16
  72.1 8.7 %fusion.38 = (f32[2,32,16,8]{3,2,1,0:T(8,128)S(1)}, f32[2,32,16,8,8]{3,4,2,1,0:T(8,128)}) fusion(f32[2,8]{1,0:T(2,128)S(1)} %get-tuple-element.31, pred[2,8]{1,0:T(4,128)(4,1)S(1)} %get-tuple-element.30, bf16[2,8,32,16,72]{4,3,0,2,1:T(8,128)(2,1)} %reshape.215, bf16[2,8,32,16,72]{4,3,0,2,1:T(8,128)(2,1)} %reshape.214), kind=kOutput, calls=%fused_computation.48 | convolution fusion | flops 9764871 | bytes 2654288 | tf_op jit(solution)/shard_map/vmap()/sub | solution.py:24
  80.8 0.0 all-to-all-done.2
  80.8 6.5 %reshape.216 = bf16[2,8,32,16,72]{4,3,0,2,1:T(8,128)(2,1)} reshape(bf16[2,1,256,1152]{3,0,1,2:T(2,128)(2,1)} %all-to-all-done.2) | data formatting | bytes 2359296 | tf_op jit(solution)/shard_map/vmap()/reshape | solution.py:17
  87.3 4.1 %convolution_bitcast_fusion.1 = bf16[2,8,32,16,72]{4,1,3,2,0:T(8,128)(2,1)S(1)} fusion(bf16[2,8,32,16,72]{4,3,0,2,1:T(8,128)(2,1)} %reshape.216, f32[2,32,16,8,8]{3,4,2,1,0:T(8,128)} %get-tuple-element.33, f32[2,32,16,8]{3,2,1,0:T(8,128)S(1)} %get-tuple-element.32), kind=kOutput, calls=%fused_computation.13 | convolution fusion | flops 9568256 | bytes 2654208 | tf_op jit(solution)/shard_map/vmap(phft,tphd->fphd)/dot_general | solution.py:27
  91.4 1.7 copy.107
  93.1 4.6 %reshape.203 = bf16[2,8,32,1152]{3,2,1,0:T(8,128)(2,1)} reshape(bf16[2,8,32,16,72]{4,3,2,1,0:T(8,128)(2,1)} %copy.107) | data formatting | bytes 2359296 | tf_op jit(solution)/shard_map/vmap()/reshape | solution.py:28
  97.7 1.5 select_convert_fusion
  99.2 0.1 copy.108
  99.4 0.0 copy-start.4
  99.4 20.7 %all_to_all.81 = bf16[2,8,32,1152]{3,2,0,1:T(8,128)(2,1)S(1)} all-to-all(bf16[2,8,32,1152]{3,2,0,1:T(8,128)(2,1)S(1)} %copy.108), channel_id=1, replica_groups=mesh['seq'=8,'rep'=4] {'seq'}, dimensions={1} | all-to-all | bytes 2359296 | tf_op jit(solution)/shard_map/all_to_all | solution.py:94
  120.1 0.1 copy.109
  120.2 0.0 copy-start.1
  120.2 1.0 copy-done.1
  121.2 4.1 %convolution_bitcast_fusion = f32[1152,1152]{0,1:T(8,128)} fusion(bf16[512,1152]{1,0:T(8,128)(2,1)S(1)} %bitcast.59, bf16[512,1152]{1,0:T(8,128)(2,1)S(1)} %bitcast.64), kind=kOutput, calls=%fused_computation.1 | convolution fusion | flops 1358954496 | bytes 7667712 | tf_op jit(solution)/shard_map/dot_general | solution.py:67
  125.3 6.9 %copy.137 = f32[1152,1152]{1,0:T(8,128)} copy(f32[1152,1152]{0,1:T(8,128)} %convolution_bitcast_fusion) | data formatting | bytes 10616832
  132.2 0.0 reduce-scatter.4.cloned.1.call-update
  132.2 0.1 compare_and_fusion
  132.3 3.1 %fusion.3 = bf16[2,1,256,1152]{3,2,0,1:T(8,128)(2,1)S(1)} fusion(bf16[1152,1152]{1,0:T(8,128)(2,1)S(1)} %copy-done, bf16[2,1,256,1152]{3,2,1,0:T(8,128)(2,1)} %param.10, pred[2,256]{1,0:T(4,128)(4,1)S(1)} %compare_and_fusion), kind=kOutput, calls=%fused_computation.10 | convolution fusion | flops 1360134144 | bytes 5014016 | tf_op jit(solution)/shard_map/dot_general | solution.py:104
  135.4 1.2 copy.110
  136.7 19.9 %all_to_all.82 = bf16[2,1,256,1152]{3,0,1,2:T(2,128)(2,1)} all-to-all(bf16[2,1,256,1152]{3,0,1,2:T(2,128)(2,1)S(1)} %copy.110), channel_id=1, replica_groups=mesh['seq'=8,'rep'=4] {'seq'}, dimensions={2} | all-to-all | bytes 2359296 | tf_op jit(solution)/shard_map/all_to_all | solution.py:108
  156.5 6.5 %reshape.217 = bf16[2,8,32,16,72]{4,3,0,2,1:T(8,128)(2,1)} reshape(bf16[2,1,256,1152]{3,0,1,2:T(2,128)(2,1)} %all_to_all.82) | data formatting | bytes 2359296 | tf_op jit(solution)/shard_map/vmap()/reshape | solution.py:39
  163.0 4.7 %convert_bitcast_fusion = bf16[2,8,32,16,72]{4,1,3,2,0:T(8,128)(2,1)S(1)} fusion(bf16[2,8,32,16,72]{4,3,0,2,1:T(8,128)(2,1)} %reshape.217, f32[2,32,16,8,8]{3,4,2,1,0:T(8,128)} %get-tuple-element.33, f32[2,32,16,8]{3,2,1,0:T(8,128)S(1)} %get-tuple-element.32), kind=kOutput, calls=%fused_computation.14 | convolution fusion | flops 10158080 | bytes 2654208 | tf_op jit(solution)/shard_map/vmap(phft,fphd->tphd)/dot_general | solution.py:41
  167.8 1.8 copy.136
  169.5 4.6 %reshape.211 = bf16[2,8,32,1152]{3,2,0,1:T(8,128)(2,1)} reshape(bf16[2,8,32,16,72]{4,3,2,0,1:T(8,128)(2,1)} %copy.136) | data formatting | bytes 2359296 | tf_op jit(solution)/shard_map/vmap()/convert_element_type | solution.py:61
  174.2 4.5 %all-to-all-start.7 = ((bf16[2,8,32,1152]{3,2,0,1:T(8,128)(2,1)}), bf16[2,8,32,1152]{3,2,0,1:T(8,128)(2,1)}, u32[]{:S(2)}, u32[]{:S(2)}) async-start(bf16[2,8,32,1152]{3,2,0,1:T(8,128)(2,1)} %reshape.211), calls=%async_computation.7 | async-start | bytes 2359296 | tf_op jit(solution)/shard_map/all_to_all | solution.py:115
  178.6 9.1 %multiply_reduce_fusion = (f32[2,32,16,8]{3,2,1,0:T(8,128)S(1)}, f32[2,32,16,8,8]{3,4,2,1,0:T(8,128)}) fusion(f32[2,32,16,8,8]{3,4,2,1,0:T(8,128)} %get-tuple-element.33, f32[2,32,16,8]{3,2,1,0:T(8,128)S(1)} %get-tuple-element.32, bf16[2,8,32,16,72]{4,3,0,2,1:T(8,128)(2,1)} %reshape.216, bf16[2,8,32,16,72]{4,3,0,2,1:T(8,128)(2,1)} %reshape.217), kind=kOutput, calls=%fused_computation.3 | convolution fusion | flops 9625600 | bytes 2949120 | tf_op jit(solution)/shard_map/vmap(fphd,tphd->phft)/dot_general | solution.py:44
  187.7 7.4 %convert_bitcast_fusion.1 = bf16[2,8,32,16,72]{4,1,3,2,0:T(8,128)(2,1)S(1)} fusion(bf16[2,8,32,16,72]{4,3,0,2,1:T(8,128)(2,1)S(1)} %copy-done.3, f32[2,32,16,8,8]{3,4,2,1,0:T(8,128)} %get-tuple-element.35, f32[2,32,16,8]{3,2,1,0:T(8,128)S(1)} %get-tuple-element.34, f32[2,32,16,8,8]{3,4,2,1,0:T(8,128)S(1)} %copy-done.7, ...), kind=kOutput, calls=%fused_computation.15 | convolution fusion | flops 57475072 | bytes 2949120 | tf_op jit(solution)/shard_map/vmap(phft,fphd->tphd)/dot_general | solution.py:54
  195.2 1.9 copy.135
  197.0 4.6 %reshape.210 = bf16[2,8,32,1152]{3,2,0,1:T(8,128)(2,1)} reshape(bf16[2,8,32,16,72]{4,3,2,0,1:T(8,128)(2,1)} %copy.135) | data formatting | bytes 2359296 | tf_op jit(solution)/shard_map/vmap()/convert_element_type | solution.py:60
  201.6 0.0 all-to-all-done.7
  201.6 4.5 %all-to-all-start.6 = ((bf16[2,8,32,1152]{3,2,0,1:T(8,128)(2,1)}), bf16[2,8,32,1152]{3,2,0,1:T(8,128)(2,1)}, u32[]{:S(2)}, u32[]{:S(2)}) async-start(bf16[2,8,32,1152]{3,2,0,1:T(8,128)(2,1)} %reshape.210), calls=%async_computation.6 | async-start | bytes 2359296 | tf_op jit(solution)/shard_map/all_to_all | solution.py:114
  206.1 8.3 %convert_bitcast_fusion.2 = bf16[2,8,32,16,72]{4,1,3,2,0:T(8,128)(2,1)S(1)} fusion(bf16[2,8,32,16,72]{4,3,0,2,1:T(8,128)(2,1)} %reshape.215, f32[2,32,16,8,8]{3,4,2,1,0:T(8,128)} %get-tuple-element.35, f32[2,32,16,8]{3,2,1,0:T(8,128)} %copy-done.8, f32[2,32,16,8,8]{3,4,2,1,0:T(8,128)} %get-tuple-element.33, f32[2,32,16,8]{3,2,1,0:T(8,128)S(1)} %get-tuple-element.32), kind=kOutput, calls=%fused_computation.16 | convolution fusion | flops 57475072 | bytes 2949120 | tf_op jit(solution)/shard_map/vmap(phft,tphd->fphd)/dot_general | solution.py:51
  214.4 1.8 copy.134
  216.2 4.6 %reshape.209 = bf16[2,8,32,1152]{3,2,0,1:T(8,128)(2,1)} reshape(bf16[2,8,32,16,72]{4,3,2,0,1:T(8,128)(2,1)} %copy.134) | data formatting | bytes 2359296 | tf_op jit(solution)/shard_map/vmap()/convert_element_type | solution.py:59
  220.8 2.2 all-to-all-done.6
  222.9 4.3 %all-to-all-start.5 = ((bf16[2,8,32,1152]{3,2,0,1:T(8,128)(2,1)}), bf16[2,8,32,1152]{3,2,0,1:T(8,128)(2,1)}, u32[]{:S(2)}, u32[]{:S(2)}) async-start(bf16[2,8,32,1152]{3,2,0,1:T(8,128)(2,1)} %reshape.209), calls=%async_computation.5 | async-start | bytes 2359296 | tf_op jit(solution)/shard_map/all_to_all | solution.py:113
  227.2 0.0 all-reduce.2.cloned.1.call-start
  227.3 0.0 reduce-scatter.4.cloned.1.call-done
  227.3 2.5 copy.138
  229.8 0.0 all-reduce.2.cloned.1.call-update
  229.8 2.4 copy.126
  232.2 2.4 copy.122
  234.6 9.5 %all-to-all-done.5 = bf16[2,8,32,1152]{3,2,0,1:T(8,128)(2,1)} async-done(((bf16[2,8,32,1152]{3,2,0,1:T(8,128)(2,1)}), bf16[2,8,32,1152]{3,2,0,1:T(8,128)(2,1)}, u32[]{:S(2)}, u32[]{:S(2)}) %all-to-all-start.5) | async-done | bytes 1179680 | tf_op jit(solution)/shard_map/all_to_all | solution.py:113
  244.0 2.5 copy.118
  246.5 2.9 convolution_convert_fusion
  249.4 39.1 %all-reduce.2.cloned.1.call-done = f32[144,1152]{0,1:T(8,128)} async-done(((f32[144,1152]{0,1:T(8,128)}), f32[144,1152]{0,1:T(8,128)}) %all-reduce.2.cloned.1.call-update) | async-done | bytes 663568 | tf_op jit(solution)/shard_map/psum | solution.py:74
  288.5 2.4 copy.131
  (14 shorter events, 0.0 us)
Async XLA Ops:
  7.2 125.2 %copy-start = (bf16[1152,1152]{1,0:T(8,128)(2,1)S(1)}, bf16[1152,1152]{1,0:T(8,128)(2,1)}, u32[]{:S(2)}) copy-start(bf16[1152,1152]{1,0:T(8,128)(2,1)} %param.11) | copy-start | bytes 7962628
  10.8 22.1 %all-to-all-start = ((bf16[2,1,256,1152]{3,0,1,2:T(2,128)(2,1)}), bf16[2,1,256,1152]{3,0,1,2:T(2,128)(2,1)}, u32[]{:S(2)}, u32[]{:S(2)}) async-start(bf16[2,1,256,1152]{3,0,1,2:T(2,128)(2,1)} %copy.97), calls=%async_computation | async-start | bytes 2359296 | tf_op jit(solution)/shard_map/all_to_all | solution.py:81
  32.9 21.1 %all-to-all-start.1 = ((bf16[2,1,256,1152]{3,0,1,2:T(2,128)(2,1)}), bf16[2,1,256,1152]{3,0,1,2:T(2,128)(2,1)}, u32[]{:S(2)}, u32[]{:S(2)}) async-start(bf16[2,1,256,1152]{3,0,1,2:T(2,128)(2,1)} %copy.99), calls=%async_computation.1 | async-start | bytes 2359296 | tf_op jit(solution)/shard_map/all_to_all | solution.py:82
  37.2 21.6 %copy-start.6 = (s32[2]{0:T(128)S(1)}, s32[2]{0:T(128)}, u32[]{:S(2)}) copy-start(s32[2]{0:T(128)} %param.13) | copy-start | bytes 28
  37.2 21.7 %copy-start.5 = (s32[2]{0:T(128)S(1)}, s32[2]{0:T(128)}, u32[]{:S(2)}) copy-start(s32[2]{0:T(128)} %param.12) | copy-start | bytes 28
  54.0 26.8 %all-to-all-start.2 = ((bf16[2,1,256,1152]{3,0,1,2:T(2,128)(2,1)}), bf16[2,1,256,1152]{3,0,1,2:T(2,128)(2,1)}, u32[]{:S(2)}, u32[]{:S(2)}) async-start(bf16[2,1,256,1152]{3,0,1,2:T(2,128)(2,1)} %copy.103), calls=%async_computation.2 | async-start | bytes 2359296 | tf_op jit(solution)/shard_map/all_to_all | solution.py:83
  58.2 169.0 %reduce-scatter.4.cloned.1.call-start = ((), (), s32[]{:S(2)}) async-start(), calls=%async_computation.10 | async-start | bytes 5971968
  99.4 21.8 %copy-start.4 = (bf16[2,1,256,1152]{3,2,1,0:T(8,128)(2,1)S(1)}, bf16[2,1,256,1152]{3,2,1,0:T(8,128)(2,1)}, u32[]{:S(2)}) copy-start(bf16[2,1,256,1152]{3,2,1,0:T(8,128)(2,1)} %param.10) | copy-start | bytes 3538948
  120.2 1.0 copy-start.1
  174.2 27.5 %all-to-all-start.7 = ((bf16[2,8,32,1152]{3,2,0,1:T(8,128)(2,1)}), bf16[2,8,32,1152]{3,2,0,1:T(8,128)(2,1)}, u32[]{:S(2)}, u32[]{:S(2)}) async-start(bf16[2,8,32,1152]{3,2,0,1:T(8,128)(2,1)} %reshape.211), calls=%async_computation.7 | async-start | bytes 2359296 | tf_op jit(solution)/shard_map/all_to_all | solution.py:115
  178.6 9.1 %copy-start.3 = (bf16[2,8,32,16,72]{4,3,0,2,1:T(8,128)(2,1)S(1)}, bf16[2,8,32,16,72]{4,3,0,2,1:T(8,128)(2,1)}, u32[]{:S(2)}) copy-start(bf16[2,8,32,16,72]{4,3,0,2,1:T(8,128)(2,1)} %reshape.214) | copy-start | bytes 3538948
  178.6 9.1 %copy-start.7 = (f32[2,32,16,8,8]{3,4,2,1,0:T(8,128)S(1)}, f32[2,32,16,8,8]{3,4,2,1,0:T(8,128)}, u32[]{:S(2)}) copy-start(f32[2,32,16,8,8]{3,4,2,1,0:T(8,128)} %get-tuple-element.33) | copy-start | bytes 786436
  187.7 7.4 %copy-start.8 = (f32[2,32,16,8]{3,2,1,0:T(8,128)}, f32[2,32,16,8]{3,2,1,0:T(8,128)S(1)}, u32[]{:S(2)}) copy-start(f32[2,32,16,8]{3,2,1,0:T(8,128)S(1)} %get-tuple-element.34) | copy-start | bytes 98308
  201.6 21.3 %all-to-all-start.6 = ((bf16[2,8,32,1152]{3,2,0,1:T(8,128)(2,1)}), bf16[2,8,32,1152]{3,2,0,1:T(8,128)(2,1)}, u32[]{:S(2)}, u32[]{:S(2)}) async-start(bf16[2,8,32,1152]{3,2,0,1:T(8,128)(2,1)} %reshape.210), calls=%async_computation.6 | async-start | bytes 2359296 | tf_op jit(solution)/shard_map/all_to_all | solution.py:114
  222.9 21.1 %all-to-all-start.5 = ((bf16[2,8,32,1152]{3,2,0,1:T(8,128)(2,1)}), bf16[2,8,32,1152]{3,2,0,1:T(8,128)(2,1)}, u32[]{:S(2)}, u32[]{:S(2)}) async-start(bf16[2,8,32,1152]{3,2,0,1:T(8,128)(2,1)} %reshape.209), calls=%async_computation.5 | async-start | bytes 2359296 | tf_op jit(solution)/shard_map/all_to_all | solution.py:113
  227.2 61.3 %all-reduce.2.cloned.1.call-start = ((), (), s32[]{:S(2)}) async-start(), calls=%async_computation.9 | async-start | bytes 2359296 | tf_op jit(solution)/shard_map/psum | solution.py:74
  244.0 2.5 copy-start.2
Sparse Core Ops, SparseCore 0:
  132.3 65.9 reduce-scatter.3
  230.4 58.0 all-reduce.1
where the time goes:
time: 303 us; the launch traced here: 298 us
  local copies, waits for them, and re-layouts  83.8 us (28%)
  waiting for transfers between devices  77.4 us (26%)
  matrix products  52.4 us (17%)
  blocking collectives  40.6 us (13%)
  starting transfers between devices  27.5 us (9%)
  between operations  14.5 us (5%)
    psum x1, waiting for transfers between devices, reduce_weight(): return lax.psum(mine, 'rep')  39.1 us
    unnamed x24, local copies, waits for them, and re-layouts  23.5 us
    all_to_all x1, blocking collectives, shards(): lax.all_to_all(attn_pos, 'seq', split_axis=1, concat_axis=2, tiled=True)  20.7 us
    all_to_all x1, blocking collectives, shards(): lax.all_to_all(out_cot, 'seq', split_axis=2, concat_axis=1, tiled=True)  19.9 us
    all_to_all x1, waiting for transfers between devices, shards(): lax.all_to_all(query_rows, 'seq', split_axis=2, concat_axis=1, tiled=True)  13.4 us
    all_to_all x1, waiting for transfers between devices, shards(): lax.all_to_all(key_rows, 'seq', split_axis=2, concat_axis=1, tiled=True)  13.3 us
    all_to_all x1, waiting for transfers between devices, shards(): lax.all_to_all(grad_query_pos, 'seq', split_axis=1, concat_axis=2, tiled=...  9.45 us
    dot_general x1, matrix products, attend_back(): jnp.einsum('fphd,tphd->phft', cot_heads, value_heads, preferred_element_t...  9.06 us
  transfers between devices with their start and end apart: 8, of which 5 were waited for; matrix products, arithmetic and copies ran while one was open for 34% of the time, Pallas kernels for 0%

commit v1 on v0

--- a/solution.py
+++ b/solution.py
@@ -71,7 +71,7 @@
         scatter_dimension=0,
         tiled=True,
     )
-    return lax.psum(mine, "rep")
+    return jnp.sum(lax.all_gather(mine, "rep"), axis=0)
 
 
 def shards(query_rows, key_rows, value_rows, out_grad, out_weight, frame_count, pos_count):

time: 303 us -> 286 us (0.944)
  waiting for transfers between devices: 77.4 us -> 60.7 us
  local copies, waits for them, and re-layouts: 83.8 us -> 78.8 us
    psum x1 -> x0, waiting for transfers between devices: 39.1 us -> none  [reduce_weight(): return lax.psum(mine, 'rep')]
    reduce_scatter x0 -> x1, waiting for transfers between devices: none -> 19.8 us  [reduce_weight(): lax.psum_scatter(lax.dot_general(flat_grad, flat_out, (((0,), (0,)), ((),...]
    unnamed x24 -> x22, local copies, waits for them, and re-layouts: 23.5 us -> 18.6 us
  transfers between devices with their start and end apart: 8 -> 8, of which waited for: 5 -> 5; matrix products, arithmetic and copies ran while one was open for 34% -> 35% of each run, Pallas kernels for 0% -> 0%
where the time goes in v1:
time: 286 us; the launch traced here: 281 us
  local copies, waits for them, and re-layouts  78.8 us (28%)
  waiting for transfers between devices  60.7 us (21%)
  matrix products  52.6 us (18%)
  blocking collectives  40.6 us (14%)
  starting transfers between devices  29.3 us (10%)
  between operations  14.5 us (5%)
  other arithmetic  4.65 us (2%)
    all_to_all x1, blocking collectives, shards(): lax.all_to_all(attn_pos, 'seq', split_axis=1, concat_axis=2, tiled=True)  20.7 us
    all_to_all x1, blocking collectives, shards(): lax.all_to_all(out_cot, 'seq', split_axis=2, concat_axis=1, tiled=True)  19.9 us
    reduce_scatter x1, waiting for transfers between devices, reduce_weight(): lax.psum_scatter(lax.dot_general(flat_grad, flat_out, (((0,), (0,)), ((),...  19.8 us
    unnamed x22, local copies, waits for them, and re-layouts  18.6 us
    all_to_all x1, waiting for transfers between devices, shards(): lax.all_to_all(query_rows, 'seq', split_axis=2, concat_axis=1, tiled=True)  13.4 us
    all_to_all x1, waiting for transfers between devices, shards(): lax.all_to_all(key_rows, 'seq', split_axis=2, concat_axis=1, tiled=True)  13.3 us
    all_to_all x1, waiting for transfers between devices, shards(): lax.all_to_all(grad_query_pos, 'seq', split_axis=1, concat_axis=2, tiled=...  12 us
    dot_general x1, matrix products, attend_back(): jnp.einsum('fphd,tphd->phft', cot_heads, value_heads, preferred_element_t...  9.03 us
  transfers between devices with their start and end apart: 8, of which 5 were waited for; matrix products, arithmetic and copies ran while one was open for 35% of the time, Pallas kernels for 0%

profile of v1, /device:TPU:0, one launch (start us, length us, event | category | flops | bytes accessed | tf_op | source)
XLA Modules:
  0.0 281.2 jit_solution(15724698330337288817)
XLA Ops:
  7.2 0.0 copy-start
  7.2 3.6 %copy.96 = bf16[2,1,256,1152]{3,0,1,2:T(2,128)(2,1)} copy(bf16[2,1,256,1152]{3,2,1,0:T(8,128)(2,1)} %param.7) | data formatting | bytes 2359296 | tf_op args[0]
  10.8 5.2 %all-to-all-start = ((bf16[2,1,256,1152]{3,0,1,2:T(2,128)(2,1)}), bf16[2,1,256,1152]{3,0,1,2:T(2,128)(2,1)}, u32[]{:S(2)}, u32[]{:S(2)}) async-start(bf16[2,1,256,1152]{3,0,1,2:T(2,128)(2,1)} %copy.96), calls=%async_computation | async-start | bytes 2359296 | tf_op jit(solution)/shard_map/all_to_all | solution.py:81
  16.0 3.5 %copy.98 = bf16[2,1,256,1152]{3,0,1,2:T(2,128)(2,1)} copy(bf16[2,1,256,1152]{3,2,1,0:T(8,128)(2,1)} %param.8) | data formatting | bytes 2359296 | tf_op args[1]
  19.5 13.4 %all-to-all-done = bf16[2,1,256,1152]{3,0,1,2:T(2,128)(2,1)} async-done(((bf16[2,1,256,1152]{3,0,1,2:T(2,128)(2,1)}), bf16[2,1,256,1152]{3,0,1,2:T(2,128)(2,1)}, u32[]{:S(2)}, u32[]{:S(2)}) %all-to-all-start) | async-done | bytes 1179680 | tf_op jit(solution)/shard_map/all_to_all | solution.py:81
  32.9 4.3 %all-to-all-start.1 = ((bf16[2,1,256,1152]{3,0,1,2:T(2,128)(2,1)}), bf16[2,1,256,1152]{3,0,1,2:T(2,128)(2,1)}, u32[]{:S(2)}, u32[]{:S(2)}) async-start(bf16[2,1,256,1152]{3,0,1,2:T(2,128)(2,1)} %copy.98), calls=%async_computation.1 | async-start | bytes 2359296 | tf_op jit(solution)/shard_map/all_to_all | solution.py:82
  37.2 0.0 copy-start.6
  37.2 0.0 copy-start.5
  37.2 3.5 %copy.102 = bf16[2,1,256,1152]{3,0,1,2:T(2,128)(2,1)} copy(bf16[2,1,256,1152]{3,2,1,0:T(8,128)(2,1)} %param.9) | data formatting | bytes 2359296 | tf_op args[2]
  40.7 13.3 %all-to-all-done.1 = bf16[2,1,256,1152]{3,0,1,2:T(2,128)(2,1)} async-done(((bf16[2,1,256,1152]{3,0,1,2:T(2,128)(2,1)}), bf16[2,1,256,1152]{3,0,1,2:T(2,128)(2,1)}, u32[]{:S(2)}, u32[]{:S(2)}) %all-to-all-start.1) | async-done | bytes 1179680 | tf_op jit(solution)/shard_map/all_to_all | solution.py:82
  54.0 4.3 %all-to-all-start.2 = ((bf16[2,1,256,1152]{3,0,1,2:T(2,128)(2,1)}), bf16[2,1,256,1152]{3,0,1,2:T(2,128)(2,1)}, u32[]{:S(2)}, u32[]{:S(2)}) async-start(bf16[2,1,256,1152]{3,0,1,2:T(2,128)(2,1)} %copy.102), calls=%async_computation.2 | async-start | bytes 2359296 | tf_op jit(solution)/shard_map/all_to_all | solution.py:83
  58.3 0.6 reduce-scatter.4.cloned.1.call-start
  58.8 0.0 copy-done.6
  58.8 0.1 broadcast_compare_fusion
  58.9 0.0 copy-done.5
  58.9 0.1 iota_compare_fusion
  59.0 0.1 broadcast_and_fusion
  59.1 6.5 %reshape.215 = bf16[2,8,32,16,72]{4,3,0,2,1:T(8,128)(2,1)} reshape(bf16[2,1,256,1152]{3,0,1,2:T(2,128)(2,1)} %all-to-all-done) | data formatting | bytes 2359296 | tf_op jit(solution)/shard_map/vmap()/reshape | solution.py:15
  65.6 6.5 %reshape.216 = bf16[2,8,32,16,72]{4,3,0,2,1:T(8,128)(2,1)} reshape(bf16[2,1,256,1152]{3,0,1,2:T(2,128)(2,1)} %all-to-all-done.1) | data formatting | bytes 2359296 | tf_op jit(solution)/shard_map/vmap()/reshape | solution.py:16
  72.1 8.7 %fusion.38 = (f32[2,32,16,8]{3,2,1,0:T(8,128)S(1)}, f32[2,32,16,8,8]{3,4,2,1,0:T(8,128)}) fusion(f32[2,8]{1,0:T(2,128)S(1)} %get-tuple-element.31, pred[2,8]{1,0:T(4,128)(4,1)S(1)} %get-tuple-element.30, bf16[2,8,32,16,72]{4,3,0,2,1:T(8,128)(2,1)} %reshape.216, bf16[2,8,32,16,72]{4,3,0,2,1:T(8,128)(2,1)} %reshape.215), kind=kOutput, calls=%fused_computation.48 | convolution fusion | flops 9764871 | bytes 2654288 | tf_op jit(solution)/shard_map/vmap()/sub | solution.py:24
  80.8 0.0 all-to-all-done.2
  80.9 6.5 %reshape.217 = bf16[2,8,32,16,72]{4,3,0,2,1:T(8,128)(2,1)} reshape(bf16[2,1,256,1152]{3,0,1,2:T(2,128)(2,1)} %all-to-all-done.2) | data formatting | bytes 2359296 | tf_op jit(solution)/shard_map/vmap()/reshape | solution.py:17
  87.4 4.1 %convolution_bitcast_fusion.1 = bf16[2,8,32,16,72]{4,1,3,2,0:T(8,128)(2,1)S(1)} fusion(bf16[2,8,32,16,72]{4,3,0,2,1:T(8,128)(2,1)} %reshape.217, f32[2,32,16,8,8]{3,4,2,1,0:T(8,128)} %get-tuple-element.33, f32[2,32,16,8]{3,2,1,0:T(8,128)S(1)} %get-tuple-element.32), kind=kOutput, calls=%fused_computation.13 | convolution fusion | flops 9568256 | bytes 2654208 | tf_op jit(solution)/shard_map/vmap(phft,tphd->fphd)/dot_general | solution.py:27
  91.4 1.7 copy.106
  93.2 4.6 %reshape.203 = bf16[2,8,32,1152]{3,2,1,0:T(8,128)(2,1)} reshape(bf16[2,8,32,16,72]{4,3,2,1,0:T(8,128)(2,1)} %copy.106) | data formatting | bytes 2359296 | tf_op jit(solution)/shard_map/vmap()/reshape | solution.py:28
  97.7 1.5 select_convert_fusion
  99.3 0.1 copy.107
  99.4 0.0 copy-start.4
  99.4 20.7 %all_to_all.81 = bf16[2,8,32,1152]{3,2,0,1:T(8,128)(2,1)S(1)} all-to-all(bf16[2,8,32,1152]{3,2,0,1:T(8,128)(2,1)S(1)} %copy.107), channel_id=1, replica_groups=mesh['seq'=8,'rep'=4] {'seq'}, dimensions={1} | all-to-all | bytes 2359296 | tf_op jit(solution)/shard_map/all_to_all | solution.py:94
  120.2 0.1 copy.108
  120.3 0.0 copy-start.1
  120.3 1.0 copy-done.1
  121.3 4.1 %convolution_bitcast_fusion = f32[1152,1152]{0,1:T(8,128)} fusion(bf16[512,1152]{1,0:T(8,128)(2,1)S(1)} %bitcast.60, bf16[512,1152]{1,0:T(8,128)(2,1)S(1)} %bitcast.66), kind=kOutput, calls=%fused_computation.1 | convolution fusion | flops 1358954496 | bytes 7667712 | tf_op jit(solution)/shard_map/dot_general | solution.py:67
  125.4 6.9 %copy.136 = f32[1152,1152]{1,0:T(8,128)} copy(f32[1152,1152]{0,1:T(8,128)} %convolution_bitcast_fusion) | data formatting | bytes 10616832
  132.3 0.0 reduce-scatter.4.cloned.1.call-update
  132.3 0.1 compare_and_fusion
  132.4 3.1 %fusion.3 = bf16[2,1,256,1152]{3,2,0,1:T(8,128)(2,1)S(1)} fusion(bf16[1152,1152]{1,0:T(8,128)(2,1)S(1)} %copy-done, bf16[2,1,256,1152]{3,2,1,0:T(8,128)(2,1)} %param.10, pred[2,256]{1,0:T(4,128)(4,1)S(1)} %compare_and_fusion), kind=kOutput, calls=%fused_computation.10 | convolution fusion | flops 1360134144 | bytes 5014016 | tf_op jit(solution)/shard_map/dot_general | solution.py:104
  135.5 1.2 copy.109
  136.7 19.9 %all_to_all.82 = bf16[2,1,256,1152]{3,0,1,2:T(2,128)(2,1)} all-to-all(bf16[2,1,256,1152]{3,0,1,2:T(2,128)(2,1)S(1)} %copy.109), channel_id=1, replica_groups=mesh['seq'=8,'rep'=4] {'seq'}, dimensions={2} | all-to-all | bytes 2359296 | tf_op jit(solution)/shard_map/all_to_all | solution.py:108
  156.6 6.5 %reshape.218 = bf16[2,8,32,16,72]{4,3,0,2,1:T(8,128)(2,1)} reshape(bf16[2,1,256,1152]{3,0,1,2:T(2,128)(2,1)} %all_to_all.82) | data formatting | bytes 2359296 | tf_op jit(solution)/shard_map/vmap()/reshape | solution.py:39
  163.1 4.7 %convert_bitcast_fusion = bf16[2,8,32,16,72]{4,1,3,2,0:T(8,128)(2,1)S(1)} fusion(bf16[2,8,32,16,72]{4,3,0,2,1:T(8,128)(2,1)} %reshape.218, f32[2,32,16,8,8]{3,4,2,1,0:T(8,128)} %get-tuple-element.33, f32[2,32,16,8]{3,2,1,0:T(8,128)S(1)} %get-tuple-element.32), kind=kOutput, calls=%fused_computation.14 | convolution fusion | flops 10158080 | bytes 2654208 | tf_op jit(solution)/shard_map/vmap(phft,fphd->tphd)/dot_general | solution.py:41
  167.9 1.8 copy.135
  169.7 4.6 %reshape.212 = bf16[2,8,32,1152]{3,2,0,1:T(8,128)(2,1)} reshape(bf16[2,8,32,16,72]{4,3,2,0,1:T(8,128)(2,1)} %copy.135) | data formatting | bytes 2359296 | tf_op jit(solution)/shard_map/vmap()/convert_element_type | solution.py:61
  174.3 4.3 %all-to-all-start.7 = ((bf16[2,8,32,1152]{3,2,0,1:T(8,128)(2,1)}), bf16[2,8,32,1152]{3,2,0,1:T(8,128)(2,1)}, u32[]{:S(2)}, u32[]{:S(2)}) async-start(bf16[2,8,32,1152]{3,2,0,1:T(8,128)(2,1)} %reshape.212), calls=%async_computation.7 | async-start | bytes 2359296 | tf_op jit(solution)/shard_map/all_to_all | solution.py:115
  178.5 0.3 all-gather.3.cloned.1.call-start
  178.8 19.8 %reduce-scatter.4.cloned.1.call-done = f32[144,1152]{1,0:T(8,128)} async-done(((f32[1152,1152]{1,0:T(8,128)}), f32[144,1152]{1,0:T(8,128)}) %reduce-scatter.4.cloned.1.call-update) | async-done | bytes 663568 | tf_op jit(solution)/shard_map/reduce_scatter | solution.py:66
  198.6 0.0 all-gather.3.cloned.1.call-update
  198.6 9.0 %multiply_reduce_fusion = (f32[2,32,16,8]{3,2,1,0:T(8,128)S(1)}, f32[2,32,16,8,8]{3,4,2,1,0:T(8,128)}) fusion(f32[2,32,16,8,8]{3,4,2,1,0:T(8,128)} %get-tuple-element.33, f32[2,32,16,8]{3,2,1,0:T(8,128)S(1)} %get-tuple-element.32, bf16[2,8,32,16,72]{4,3,0,2,1:T(8,128)(2,1)} %reshape.217, bf16[2,8,32,16,72]{4,3,0,2,1:T(8,128)(2,1)} %reshape.218), kind=kOutput, calls=%fused_computation.3 | convolution fusion | flops 9625600 | bytes 2949120 | tf_op jit(solution)/shard_map/vmap(fphd,tphd->phft)/dot_general | solution.py:44
  207.7 7.6 %convert_bitcast_fusion.1 = bf16[2,8,32,16,72]{4,1,3,2,0:T(8,128)(2,1)S(1)} fusion(bf16[2,8,32,16,72]{4,3,0,2,1:T(8,128)(2,1)S(1)} %copy-done.3, f32[2,32,16,8,8]{3,4,2,1,0:T(8,128)} %get-tuple-element.35, f32[2,32,16,8]{3,2,1,0:T(8,128)S(1)} %get-tuple-element.34, f32[2,32,16,8,8]{3,4,2,1,0:T(8,128)S(1)} %copy-done.7, ...), kind=kOutput, calls=%fused_computation.15 | convolution fusion | flops 57475072 | bytes 2949120 | tf_op jit(solution)/shard_map/vmap(phft,fphd->tphd)/dot_general | solution.py:54
  215.3 1.8 copy.134
  217.1 4.6 %reshape.211 = bf16[2,8,32,1152]{3,2,0,1:T(8,128)(2,1)} reshape(bf16[2,8,32,16,72]{4,3,2,0,1:T(8,128)(2,1)} %copy.134) | data formatting | bytes 2359296 | tf_op jit(solution)/shard_map/vmap()/convert_element_type | solution.py:60
  221.7 0.0 all-to-all-done.7
  221.7 6.3 %all-to-all-start.6 = ((bf16[2,8,32,1152]{3,2,0,1:T(8,128)(2,1)}), bf16[2,8,32,1152]{3,2,0,1:T(8,128)(2,1)}, u32[]{:S(2)}, u32[]{:S(2)}) async-start(bf16[2,8,32,1152]{3,2,0,1:T(8,128)(2,1)} %reshape.211), calls=%async_computation.6 | async-start | bytes 2359296 | tf_op jit(solution)/shard_map/all_to_all | solution.py:114
  228.0 8.3 %convert_bitcast_fusion.2 = bf16[2,8,32,16,72]{4,1,3,2,0:T(8,128)(2,1)S(1)} fusion(bf16[2,8,32,16,72]{4,3,0,2,1:T(8,128)(2,1)} %reshape.216, f32[2,32,16,8,8]{3,4,2,1,0:T(8,128)} %get-tuple-element.35, f32[2,32,16,8]{3,2,1,0:T(8,128)} %copy-done.8, f32[2,32,16,8,8]{3,4,2,1,0:T(8,128)} %get-tuple-element.33, f32[2,32,16,8]{3,2,1,0:T(8,128)S(1)} %get-tuple-element.32), kind=kOutput, calls=%fused_computation.16 | convolution fusion | flops 57475072 | bytes 2949120 | tf_op jit(solution)/shard_map/vmap(phft,tphd->fphd)/dot_general | solution.py:51
  236.3 1.8 copy.133
  238.0 4.6 %reshape.210 = bf16[2,8,32,1152]{3,2,0,1:T(8,128)(2,1)} reshape(bf16[2,8,32,16,72]{4,3,2,0,1:T(8,128)(2,1)} %copy.133) | data formatting | bytes 2359296 | tf_op jit(solution)/shard_map/vmap()/convert_element_type | solution.py:59
  242.6 2.2 all-to-all-done.6
  244.8 4.3 %all-to-all-start.5 = ((bf16[2,8,32,1152]{3,2,0,1:T(8,128)(2,1)}), bf16[2,8,32,1152]{3,2,0,1:T(8,128)(2,1)}, u32[]{:S(2)}, u32[]{:S(2)}) async-start(bf16[2,8,32,1152]{3,2,0,1:T(8,128)(2,1)} %reshape.210), calls=%async_computation.5 | async-start | bytes 2359296 | tf_op jit(solution)/shard_map/all_to_all | solution.py:113
  249.1 2.4 copy.125
  251.5 2.4 copy.121
  253.9 12.0 %all-to-all-done.5 = bf16[2,8,32,1152]{3,2,0,1:T(8,128)(2,1)} async-done(((bf16[2,8,32,1152]{3,2,0,1:T(8,128)(2,1)}), bf16[2,8,32,1152]{3,2,0,1:T(8,128)(2,1)}, u32[]{:S(2)}, u32[]{:S(2)}) %all-to-all-start.5) | async-done | bytes 1179680 | tf_op jit(solution)/shard_map/all_to_all | solution.py:113
  265.9 2.5 copy.117
  268.4 2.9 %convolution_convert_fusion = bf16[512,1152]{1,0:T(8,128)(2,1)} fusion(bf16[512,1152]{1,0:T(8,128)(2,1)S(1)} %bitcast.61, bf16[1152,1152]{1,0:T(8,128)(2,1)S(1)} %copy-done), kind=kOutput, calls=%fused_computation.8 | convolution fusion | flops 1359544320 | bytes 5013504 | tf_op jit(solution)/shard_map/dot_general | solution.py:97
  271.3 2.8 reduce_sum.29
  (13 shorter events, 0.0 us)
Async XLA Ops:
  7.2 125.2 %copy-start = (bf16[1152,1152]{1,0:T(8,128)(2,1)S(1)}, bf16[1152,1152]{1,0:T(8,128)(2,1)}, u32[]{:S(2)}) copy-start(bf16[1152,1152]{1,0:T(8,128)(2,1)} %param.11) | copy-start | bytes 7962628
  10.8 22.1 %all-to-all-start = ((bf16[2,1,256,1152]{3,0,1,2:T(2,128)(2,1)}), bf16[2,1,256,1152]{3,0,1,2:T(2,128)(2,1)}, u32[]{:S(2)}, u32[]{:S(2)}) async-start(bf16[2,1,256,1152]{3,0,1,2:T(2,128)(2,1)} %copy.96), calls=%async_computation | async-start | bytes 2359296 | tf_op jit(solution)/shard_map/all_to_all | solution.py:81
  32.9 21.1 %all-to-all-start.1 = ((bf16[2,1,256,1152]{3,0,1,2:T(2,128)(2,1)}), bf16[2,1,256,1152]{3,0,1,2:T(2,128)(2,1)}, u32[]{:S(2)}, u32[]{:S(2)}) async-start(bf16[2,1,256,1152]{3,0,1,2:T(2,128)(2,1)} %copy.98), calls=%async_computation.1 | async-start | bytes 2359296 | tf_op jit(solution)/shard_map/all_to_all | solution.py:82
  37.2 21.6 %copy-start.6 = (s32[2]{0:T(128)S(1)}, s32[2]{0:T(128)}, u32[]{:S(2)}) copy-start(s32[2]{0:T(128)} %param.13) | copy-start | bytes 28
  37.2 21.7 %copy-start.5 = (s32[2]{0:T(128)S(1)}, s32[2]{0:T(128)}, u32[]{:S(2)}) copy-start(s32[2]{0:T(128)} %param.12) | copy-start | bytes 28
  54.0 26.9 %all-to-all-start.2 = ((bf16[2,1,256,1152]{3,0,1,2:T(2,128)(2,1)}), bf16[2,1,256,1152]{3,0,1,2:T(2,128)(2,1)}, u32[]{:S(2)}, u32[]{:S(2)}) async-start(bf16[2,1,256,1152]{3,0,1,2:T(2,128)(2,1)} %copy.102), calls=%async_computation.2 | async-start | bytes 2359296 | tf_op jit(solution)/shard_map/all_to_all | solution.py:83
  58.3 140.3 %reduce-scatter.4.cloned.1.call-start = ((), (), s32[]{:S(2)}) async-start(), calls=%async_computation.10 | async-start | bytes 5971968 | tf_op jit(solution)/shard_map/reduce_scatter | solution.py:66
  99.4 21.9 %copy-start.4 = (bf16[2,1,256,1152]{3,2,1,0:T(8,128)(2,1)S(1)}, bf16[2,1,256,1152]{3,2,1,0:T(8,128)(2,1)}, u32[]{:S(2)}) copy-start(bf16[2,1,256,1152]{3,2,1,0:T(8,128)(2,1)} %param.10) | copy-start | bytes 3538948
  120.3 1.0 copy-start.1
  174.3 47.4 %all-to-all-start.7 = ((bf16[2,8,32,1152]{3,2,0,1:T(8,128)(2,1)}), bf16[2,8,32,1152]{3,2,0,1:T(8,128)(2,1)}, u32[]{:S(2)}, u32[]{:S(2)}) async-start(bf16[2,8,32,1152]{3,2,0,1:T(8,128)(2,1)} %reshape.212), calls=%async_computation.7 | async-start | bytes 2359296 | tf_op jit(solution)/shard_map/all_to_all | solution.py:115
  178.5 92.8 %all-gather.3.cloned.1.call-start = ((), (), s32[]{:S(2)}) async-start(), calls=%async_computation.9 | async-start | bytes 3317760 | tf_op jit(solution)/shard_map/all_gather | solution.py:74
  198.6 9.1 %copy-start.3 = (bf16[2,8,32,16,72]{4,3,0,2,1:T(8,128)(2,1)S(1)}, bf16[2,8,32,16,72]{4,3,0,2,1:T(8,128)(2,1)}, u32[]{:S(2)}) copy-start(bf16[2,8,32,16,72]{4,3,0,2,1:T(8,128)(2,1)} %reshape.215) | copy-start | bytes 3538948
  198.6 9.0 %copy-start.7 = (f32[2,32,16,8,8]{3,4,2,1,0:T(8,128)S(1)}, f32[2,32,16,8,8]{3,4,2,1,0:T(8,128)}, u32[]{:S(2)}) copy-start(f32[2,32,16,8,8]{3,4,2,1,0:T(8,128)} %get-tuple-element.33) | copy-start | bytes 786436
  207.7 7.6 %copy-start.8 = (f32[2,32,16,8]{3,2,1,0:T(8,128)}, f32[2,32,16,8]{3,2,1,0:T(8,128)S(1)}, u32[]{:S(2)}) copy-start(f32[2,32,16,8]{3,2,1,0:T(8,128)S(1)} %get-tuple-element.34) | copy-start | bytes 98308
  221.7 23.1 %all-to-all-start.6 = ((bf16[2,8,32,1152]{3,2,0,1:T(8,128)(2,1)}), bf16[2,8,32,1152]{3,2,0,1:T(8,128)(2,1)}, u32[]{:S(2)}, u32[]{:S(2)}) async-start(bf16[2,8,32,1152]{3,2,0,1:T(8,128)(2,1)} %reshape.211), calls=%async_computation.6 | async-start | bytes 2359296 | tf_op jit(solution)/shard_map/all_to_all | solution.py:114
  244.8 21.1 %all-to-all-start.5 = ((bf16[2,8,32,1152]{3,2,0,1:T(8,128)(2,1)}), bf16[2,8,32,1152]{3,2,0,1:T(8,128)(2,1)}, u32[]{:S(2)}, u32[]{:S(2)}) async-start(bf16[2,8,32,1152]{3,2,0,1:T(8,128)(2,1)} %reshape.210), calls=%async_computation.5 | async-start | bytes 2359296 | tf_op jit(solution)/shard_map/all_to_all | solution.py:113
  265.9 2.5 copy-start.2
Sparse Core Ops, SparseCore 0:
  132.4 66.1 reduce-scatter.3
  200.1 57.8 all-gather.2
